TPU v7x, 256 devices: a whole 4x4x8 slice. The times are simulated.
256 devices in a mesh: layer: 64 (over x, z_lo, y, core), tensor: 4 (over z_hi).
Axes of the slice: x: 4, y: 4, z: 8 (z_hi: 4, z_lo: 2; z = z_hi * 2 + z_lo), core: 2. Of those that a mesh axis runs over, the one named last changes fastest.
Arguments:
- gradient: bfloat16 [64, 1024, 8192], P(None, 'tensor', 'layer'), may hold values from -8 to 8
- row_basis: bfloat16 [64, 1024, 256], P('layer', 'tensor'), may hold values from -0.1875 to 0.1875
- column_basis: bfloat16 [64, 8192, 256], P('layer', 'tensor'), may hold values from -0.0625 to 0.0625
- row_eigen: float32 [64, 256], P('layer'), may hold values from 0.01 to 10
- column_eigen: float32 [64, 256], P('layer'), may hold values from 0.01 to 10
- row_escape: float32 [64], P('layer'), may hold values from 0.02 to 0.2
- column_escape: float32 [64], P('layer'), may hold values from 0.02 to 0.2
Outputs:
- update: bfloat16 [64, 1024, 8192], P(None, 'tensor', 'layer')
All inputs are finite; a program needn't handle non-finite values.
Results may differ from a plain program's by a relative error of at most 0.0055.
Values may be sent and summed in bfloat16 or wider, within the bound.
A program may use at most 128 MiB of HBM per device.

v0:
```python
import jax
import jax.numpy as jnp
from jax import lax
from jax.sharding import PartitionSpec as P


def from_everyone(value, axis):
    copies = jnp.broadcast_to(value, (lax.axis_size(axis), *value.shape))
    return lax.all_to_all(copies, axis, split_axis=0, concat_axis=0, tiled=True)


def laid_out(parts, dim):
    dims = list(parts.shape[1:])
    dims[dim] *= parts.shape[0]
    return jnp.moveaxis(parts, 0, dim).reshape(dims)


def gather_directly(value, axis, dim):
    parts = from_everyone(value, axis)
    return laid_out(parts, dim)


def split_up(value, dim, peers):
    before, after = (value.shape[:dim], value.shape[dim + 1 :])
    return jnp.moveaxis(value.reshape(*before, peers, -1, *after), dim, 0)


def edges_of(length, count):
    unit = 8 if length >= 8 * count else 1
    return [length // unit * k // count * unit for k in range(1, count)]


def cut_exchange(value, axis, pieces, split_dim, concat_dim):
    parts = split_up(value, split_dim, lax.axis_size(axis))
    cut = max(range(1, max(2, parts.ndim - 1)), key=lambda d: parts.shape[d])
    outs = []
    for section in jnp.split(parts, edges_of(parts.shape[cut], pieces), axis=cut):
        if section.size:
            outs.append(lax.all_to_all(section, axis, split_axis=0, concat_axis=0, tiled=True))
    return laid_out(jnp.concatenate(outs, axis=cut), concat_dim)


def coefficients(row_eigen, column_eigen, row_escape, column_escape):
    row_base = row_escape ** (-0.25)
    column_base = column_escape ** (-0.25)
    row_coef = (row_eigen + row_escape[:, None]) ** (-0.25) - row_base[:, None]
    column_coef = (column_eigen + column_escape[:, None]) ** (-0.25) - column_base[:, None]
    return (row_base, column_base, row_coef, column_coef)


def group_norm(local_block):
    partial_sq = jnp.sum(jnp.square(local_block.astype(jnp.float32)), axis=(1, 2))
    return lax.psum(partial_sq, "tensor")


def finish(raw_update, grad_sq):
    update_sq = lax.psum(jnp.sum(jnp.square(raw_update), axis=(1, 2)), "tensor")
    factor = jnp.sqrt((grad_sq + 1.0) / (update_sq + 1.0))
    return (raw_update * factor[:, None, None]).astype(jnp.bfloat16)


def body(gradient, row_basis, column_basis, row_eigen, column_eigen, row_escape, column_escape):
    row_base, column_base, row_coef, column_coef = coefficients(
        row_eigen, column_eigen, row_escape, column_escape
    )
    both_base = (row_base * column_base)[:, None, None]
    group_block = lax.all_to_all(gradient, "layer", split_axis=0, concat_axis=2, tiled=True)
    grad_sq = group_norm(group_block)
    own_proj = lax.psum_scatter(
        jnp.einsum(
            "lrk,lrd->dlk", row_basis, group_block, preferred_element_type=jnp.float32
        ).astype(jnp.bfloat16),
        "tensor",
        scatter_dimension=0,
        tiled=True,
    ).astype(jnp.float32)
    scaled = (own_proj * row_coef[None]).astype(jnp.bfloat16)
    core_part = jnp.einsum("dlk,ldj->lkj", scaled, column_basis, preferred_element_type=jnp.float32)
    core_mat = lax.psum(core_part.astype(jnp.bfloat16), "tensor")
    whole_columns = gather_directly(column_basis, "tensor", 1)
    middle = jnp.einsum(
        "lrd,ldk->lrk", group_block, whole_columns, preferred_element_type=jnp.float32
    )
    row_term = jnp.einsum(
        "lrk,dlk->lrd",
        row_basis,
        gather_directly(scaled, "tensor", 0),
        preferred_element_type=jnp.float32,
    )
    mixed = row_base[:, None, None] * middle + jnp.einsum(
        "lrk,lkj->lrj", row_basis, core_mat, preferred_element_type=jnp.float32
    )
    left_factor = (mixed * column_coef[:, None, :]).astype(jnp.bfloat16)
    raw_update = both_base * group_block.astype(jnp.float32) + column_base[:, None, None] * row_term
    raw_update = raw_update + jnp.einsum(
        "lrk,ldk->lrd", left_factor, whole_columns, preferred_element_type=jnp.float32
    )
    rows_block = finish(raw_update, grad_sq)
    return cut_exchange(rows_block, "layer", 2, 2, 0)


def solution(mesh):
    in_specs = (
        P(None, "tensor", "layer"),
        P("layer", "tensor", None),
        P("layer", "tensor", None),
        P("layer", None),
        P("layer", None),
        P("layer"),
        P("layer"),
    )
    out_specs = P(None, "tensor", "layer")
    return jax.shard_map(body, mesh=mesh, in_specs=in_specs, out_specs=out_specs, check_vma=False)
```

profile of v0, /device:TPU:5, one launch (start us, length us, event | category | flops | bytes accessed | tf_op | source)
XLA Modules:
  0.0 502.8 jit_solution(12771403566630581161)
XLA Ops:
  6.5 0.0 copy-start
  6.5 0.0 reduce-scatter.2.cloned.1.call-start
  6.5 58.7 %all_to_all.38 = bf16[64,256,128]{2,1,0:T(8,128)(2,1)} all-to-all(bf16[64,256,128]{2,1,0:T(8,128)(2,1)} %param.7), channel_id=1, replica_groups=mesh['layer'=64,'tensor'=4] {'layer'}, dimensions={0} | all-to-all | bytes 8388608 | tf_op jit(solution)/shard_map/all_to_all | solution.py:67
  65.2 6.4 %copy.14 = bf16[1,256,64,128]{1,3,2,0:T(8,128)(2,1)} copy(bf16[1,256,64,128]{3,1,2,0:T(8,128)(2,1)} %bitcast.66) | data formatting | bytes 8388608 | tf_op jit(solution)/shard_map/all_to_all | solution.py:67
  71.6 0.0 copy-done
  71.6 5.4 %fusion.2 = bf16[8192,1,256]{2,0,1:T(8,128)(2,1)} fusion(bf16[256,8192]{0,1:T(8,128)(2,1)} %bitcast.63, bf16[1,256,256]{2,1,0:T(8,128)(2,1)S(1)} %copy-done), kind=kOutput, calls=%fused_computation.5 | convolution fusion | flops 1075838976 | bytes 8519680 | tf_op jit(solution)/shard_map/lrk,lrd->dlk/dot_general | solution.py:70
  77.0 0.0 copy-start.2
  77.0 0.0 reduce-scatter.2.cloned.1.call-update
  77.0 1.2 copy-done.2
  78.2 2.2 broadcast_in_dim.5
  80.4 0.0 copy-start.3
  80.4 7.4 %all-to-all-start.2 = ((bf16[4,1,2048,256]{3,2,1,0:T(8,128)(2,1)}), bf16[4,1,2048,256]{3,2,1,0:T(8,128)(2,1)}, u32[]{:S(2)}, u32[]{:S(2)}) async-start(bf16[4,1,2048,256]{3,2,1,0:T(8,128)(2,1)} %broadcast_in_dim.5), calls=%async_computation.3 | async-start | bytes 8388608 | tf_op jit(solution)/shard_map/all_to_all | solution.py:9
  88.6 0.0 copy-done.3
  88.6 107.0 %reduce-scatter.2.cloned.1.call-done = bf16[2048,1,256]{2,0,1:T(8,128)(2,1)} async-done(((bf16[8192,1,256]{2,0,1:T(8,128)(2,1)}), bf16[2048,1,256]{2,0,1:T(8,128)(2,1)}) %reduce-scatter.2.cloned.1.call-update) | async-done | bytes 1048592 | tf_op jit(solution)/shard_map/reduce_scatter | solution.py:69
  195.6 1.4 fusion.6
  197.0 0.0 all-to-all-done.2
  197.1 2.2 broadcast_in_dim.4
  199.3 0.0 copy-start.4
  199.3 60.2 %all-to-all-start.1 = ((bf16[4,2048,1,256]{3,1,2,0:T(8,128)(2,1)}), bf16[4,2048,1,256]{3,1,2,0:T(8,128)(2,1)}, u32[]{:S(2)}, u32[]{:S(2)}) async-start(bf16[4,2048,1,256]{3,1,2,0:T(8,128)(2,1)} %broadcast_in_dim.4), calls=%async_computation.2 | async-start | bytes 8388608 | tf_op jit(solution)/shard_map/all_to_all | solution.py:9
  259.5 0.0 all-reduce.3.cloned.1.call-start
  259.5 0.0 copy-start.1
  260.3 0.0 copy-done.4
  260.4 5.2 %multiply_reduce_fusion.1 = f32[]{:T(128)} fusion(bf16[64,256,128]{2,1,0:T(8,128)(2,1)} %all_to_all.38), kind=kLoop, calls=%fused_computation.8 | loop fusion | flops 6291455 | bytes 4194308 | tf_op jit(solution)/shard_map/reduce_sum | solution.py:52
  265.5 0.0 copy-done.1
  265.5 3.5 convolution_multiply_fusion.1
  269.0 1.1 convolution_convert_fusion.1
  270.1 0.0 all-reduce.3.cloned.1.call-update
  270.1 50.7 %all-to-all-done.1 = bf16[4,2048,1,256]{3,1,2,0:T(8,128)(2,1)} async-done(((bf16[4,2048,1,256]{3,1,2,0:T(8,128)(2,1)}), bf16[4,2048,1,256]{3,1,2,0:T(8,128)(2,1)}, u32[]{:S(2)}, u32[]{:S(2)}) %all-to-all-start.1) | async-done | bytes 4194336 | tf_op jit(solution)/shard_map/all_to_all | solution.py:9
  320.9 8.0 %fusion.1 = f32[256,8192]{0,1:T(8,128)} fusion(bf16[8192,256]{1,0:T(8,128)(2,1)} %bitcast.11, bf16[256,8192]{0,1:T(8,128)(2,1)} %bitcast.64, f32[]{:T(128)} %bitcast.4, f32[]{:T(128)} %bitcast, bf16[1,256,256]{2,1,0:T(8,128)(2,1)S(1)} %copy-done), kind=kOutput, calls=%fused_computation.3 | convolution fusion | flops 1082130432 | bytes 16908296 | tf_op jit(solution)/shard_map/lrk,dlk->lrd/dot_general | solution.py:84
  328.9 54.9 %all-reduce.3.cloned.1.call-done = bf16[256,256]{1,0:T(8,128)(2,1)} async-done(((bf16[256,256]{1,0:T(8,128)(2,1)}), bf16[256,256]{1,0:T(8,128)(2,1)}) %all-reduce.3.cloned.1.call-update) | async-done | bytes 131088 | tf_op jit(solution)/shard_map/psum | solution.py:79
  383.8 11.0 %multiply_reduce_fusion = (f32[]{:T(128)}, f32[256,8192]{0,1:T(8,128)}) fusion(f32[256,8192]{0,1:T(8,128)} %fusion.1, bf16[8192,256]{1,0:T(8,128)(2,1)} %bitcast.14, f32[256,256]{1,0:T(8,128)S(1)} %convolution_multiply_fusion.1, bf16[256,256]{1,0:T(8,128)(2,1)} %all-reduce.3.cloned.1.call-done, bf16[1,256,256]{2,1,0:T(8,128)(2,1)S(1)} %copy-done, ...), kind=kOutput, calls=%fused_computation.7 | convolution fusion | flops 1113784320 | bytes 21496836 | tf_op jit(solution)/shard_map/lrk,ldk->lrd/dot_general | solution.py:95
  394.7 10.5 %all-reduce = (f32[1]{0:T(128)}, f32[1]{0:T(128)}) all-reduce(f32[1]{0:T(128)} %bitcast.19, f32[1]{0:T(128)} %bitcast.20), channel_id=1, replica_groups=mesh['layer'=64,'tensor'=4] {'tensor'}, use_global_device_ids=true, to_apply=%region_3.0 | all-reduce | flops 2 | bytes 16 | tf_op jit(solution)/shard_map/psum | solution.py:53
  406.5 6.1 %multiply_convert_fusion = bf16[256,8192]{0,1:T(8,128)(2,1)} fusion(f32[256,8192]{0,1:T(8,128)} %get-tuple-element.10, f32[]{:T(128)} %bitcast.21), kind=kLoop, calls=%fused_computation.6 | loop fusion | flops 4194304 | bytes 12582916 | tf_op jit(solution)/shard_map/convert_element_type | solution.py:59
  412.5 6.4 %copy.17 = bf16[1,256,64,128]{3,1,0,2:T(8,128)(2,1)} copy(bf16[1,256,64,128]{1,3,2,0:T(8,128)(2,1)} %bitcast.68) | data formatting | bytes 8388608 | tf_op jit(solution)/shard_map/reshape | solution.py:25
  418.9 2.7 fusion.13
  421.6 38.2 %all_to_all.39 = bf16[64,1,128,128]{3,2,1,0:T(8,128)(2,1)S(1)} all-to-all(bf16[64,1,128,128]{3,2,1,0:T(8,128)(2,1)S(1)} %get-tuple-element.7), channel_id=1, replica_groups=mesh['layer'=64,'tensor'=4] {'layer'}, dimensions={0} | all-to-all | bytes 4194304 | tf_op jit(solution)/shard_map/all_to_all | solution.py:39
  459.9 33.6 %all_to_all.40 = bf16[64,1,128,128]{3,2,1,0:T(8,128)(2,1)S(1)} all-to-all(bf16[64,1,128,128]{3,2,1,0:T(8,128)(2,1)S(1)} %get-tuple-element.8), channel_id=1, replica_groups=mesh['layer'=64,'tensor'=4] {'layer'}, dimensions={0} | all-to-all | bytes 4194304 | tf_op jit(solution)/shard_map/all_to_all | solution.py:39
  493.4 2.5 maximum_bitcast_fusion
  (2 shorter events, 0.0 us)
Async XLA Ops:
  6.5 65.1 %copy-start = (bf16[1,256,256]{2,1,0:T(8,128)(2,1)S(1)}, bf16[1,256,256]{2,1,0:T(8,128)(2,1)}, u32[]{:S(2)}) copy-start(bf16[1,256,256]{2,1,0:T(8,128)(2,1)} %param.8) | copy-start | bytes 393220
  6.5 189.1 %reduce-scatter.2.cloned.1.call-start = ((), (), s32[]{:S(2)}) async-start(), calls=%async_computation.6 | async-start | bytes 5242880 | tf_op jit(solution)/shard_map/reduce_scatter | solution.py:69
  77.0 1.2 copy-start.2
  80.4 8.1 %copy-start.3 = (f32[1,256]{1,0:T(1,128)S(1)}, f32[1,256]{1,0:T(1,128)}, u32[]{:S(2)}) copy-start(f32[1,256]{1,0:T(1,128)} %param.10) | copy-start | bytes 3076
  80.4 116.6 %all-to-all-start.2 = ((bf16[4,1,2048,256]{3,2,1,0:T(8,128)(2,1)}), bf16[4,1,2048,256]{3,2,1,0:T(8,128)(2,1)}, u32[]{:S(2)}, u32[]{:S(2)}) async-start(bf16[4,1,2048,256]{3,2,1,0:T(8,128)(2,1)} %broadcast_in_dim.5), calls=%async_computation.3 | async-start | bytes 8388608 | tf_op jit(solution)/shard_map/all_to_all | solution.py:9
  199.3 61.0 %copy-start.4 = (f32[1,256]{1,0:T(1,128)S(1)}, f32[1,256]{1,0:T(1,128)}, u32[]{:S(2)}) copy-start(f32[1,256]{1,0:T(1,128)} %param.11) | copy-start | bytes 3076
  199.3 121.6 %all-to-all-start.1 = ((bf16[4,2048,1,256]{3,1,2,0:T(8,128)(2,1)}), bf16[4,2048,1,256]{3,1,2,0:T(8,128)(2,1)}, u32[]{:S(2)}, u32[]{:S(2)}) async-start(bf16[4,2048,1,256]{3,1,2,0:T(8,128)(2,1)} %broadcast_in_dim.4), calls=%async_computation.2 | async-start | bytes 8388608 | tf_op jit(solution)/shard_map/all_to_all | solution.py:9
  259.5 124.3 %all-reduce.3.cloned.1.call-start = ((), (), s32[]{:S(2)}) async-start(), calls=%async_computation.7 | async-start | bytes 262144 | tf_op jit(solution)/shard_map/psum | solution.py:79
  259.5 6.0 %copy-start.1 = (bf16[1,256,64,128]{1,3,2,0:T(8,128)(2,1)S(1)}, bf16[1,256,64,128]{1,3,2,0:T(8,128)(2,1)}, u32[]{:S(2)}) copy-start(bf16[1,256,64,128]{1,3,2,0:T(8,128)(2,1)} %copy.14) | copy-start | bytes 12582916
Sparse Core Ops, SparseCore 0:
  77.1 118.4 reduce-scatter.1
  270.3 113.4 all-reduce.2
where the time goes:
time: 507 us; the launch traced here: 503 us
  waiting for transfers between devices  213 us (42%)
  blocking collectives  141 us (28%)
  starting transfers between devices  67.6 us (13%)
  matrix products  29 us (6%)
  local copies, waits for them, and re-layouts  21.1 us (4%)
  between operations  16.3 us (3%)
  other arithmetic  15.2 us (3%)
    reduce_scatter x1, waiting for transfers between devices, body(): lax.psum_scatter(jnp.einsum('lrk,lrd->dlk', row_basis, group_block, prefe...  107 us
    all_to_all x2, blocking collectives, cut_exchange(): lax.all_to_all(section, axis, split_axis=0, concat_axis=0, tiled=True)  71.8 us
    all_to_all x2, starting transfers between devices, from_everyone(): return lax.all_to_all(copies, axis, split_axis=0, concat_axis=0, tiled=True)  67.6 us
    all_to_all x1, blocking collectives, body(): lax.all_to_all(gradient, 'layer', split_axis=0, concat_axis=2, tiled=True)  58.7 us
    psum x1, waiting for transfers between devices, body(): core_mat = lax.psum(core_part.astype(jnp.bfloat16), 'tensor')  54.9 us
    all_to_all x2, waiting for transfers between devices, from_everyone(): return lax.all_to_all(copies, axis, split_axis=0, concat_axis=0, tiled=True)  50.8 us
    dot_general x1, matrix products, body(): jnp.einsum('lrk,ldk->lrd', left_factor, whole_columns, preferred_element_...  11 us
    psum x1, blocking collectives, group_norm(): return lax.psum(partial_sq, 'tensor')  10.5 us
  transfers between devices with their start and end apart: 4, of which 3 were waited for; matrix products, arithmetic and copies ran while one was open for 4% of the time, Pallas kernels for 0%

commit v1 on v0

v1 whole, which is shorter than its diff:
```python
import jax
import jax.numpy as jnp
from jax import lax
from jax.experimental import pallas as pl
from jax.experimental.pallas import tpu as pltpu
from jax.sharding import PartitionSpec as P

MESH = pl.DeviceIdType.MESH
F32 = jnp.float32
BF16 = jnp.bfloat16


def layer_at(x, y, zlo, core):
    return ((x * 2 + zlo) * 4 + y) * 2 + core


def remote(src, dst, send, recv, layer, tensor):
    return pltpu.make_async_remote_copy(
        src_ref=src,
        dst_ref=dst,
        send_sem=send,
        recv_sem=recv,
        device_id=(layer, tensor),
        device_id_type=MESH,
    )


def wait_bytes(ref, sem):
    pltpu.make_async_copy(ref, ref, sem).wait()


def inverse_fourth_root(value):
    return lax.rsqrt(jnp.sqrt(value))


def fold(value):
    rows, cols = value.shape
    parts = jnp.sum((value * value).reshape(rows // 8, 8, cols), axis=0)
    return sum(parts[:, c : c + 128] for c in range(0, cols, 128))


def kernel(
    row_esc,
    col_esc,
    grad,
    row_own,
    cols,
    row_eig,
    col_eig,
    out,
    block,
    mid,
    rows,
    rows_t,
    coef_t,
    scaled,
    middle,
    mid_send,
    mid_recv,
    mid_all,
    left,
    raw,
    ready,
    norm_send,
    norm_recv,
    grad_acc,
    sent,
    relay_sem,
    block_sem,
    rows_sem,
    rows_sent,
    part_sem,
    part_sent,
    full_sem,
    full_sent,
    norm_sem,
    norm_sent,
    out_sem,
    out_sent,
):
    me, t = lax.axis_index("layer"), lax.axis_index("tensor")
    x, zlo, y, core = me // 16, lax.rem(me // 8, 2), lax.rem(me // 2, 4), lax.rem(me, 2)
    z = 2 * t + zlo
    my_block = lax.rem(me, 16)
    home = t == x

    barrier = pltpu.get_barrier_semaphore()

    def greet_plane(i, carry):
        d = lax.rem((x * 4 + y) * 2 + core + i, 32)
        pl.semaphore_signal(
            barrier,
            inc=1,
            device_id=(layer_at(d // 8, lax.rem(d // 2, 4), zlo, lax.rem(d, 2)), t),
            device_id_type=MESH,
        )
        return carry

    def greet_ring(i, carry):
        dz = lax.rem(z + i, 8)
        pl.semaphore_signal(
            barrier,
            inc=1,
            device_id=(layer_at(x, y, lax.rem(dz, 2), core), dz // 2),
            device_id_type=MESH,
        )
        return carry

    lax.fori_loop(1, 32, greet_plane, 0)
    lax.fori_loop(1, 8, greet_ring, 0)
    pl.semaphore_wait(barrier, 38)

    def offsets(k):
        a = lax.rem(k + 1, 4)
        return a, lax.rem(k // 4 + a, 4)

    def block_rows(ref, index, part):
        return ref.at[index, pl.ds(pl.multiple_of(part * 256, 256), 256)]

    def scatter_plane(k, carry):
        kk, dest_core = lax.rem(k, 16), k // 16
        a, b = offsets(kk)
        dx, dy = lax.rem(x + a, 4), lax.rem(y + b, 4)
        mine = (dx == x) & (dy == y) & (dest_core == core)
        relay = layer_at(dx, dy, zlo, dest_core)
        slot = core * 16 + kk
        for dz in range(2):
            layer = layer_at(dx, dy, dz, dest_core)
            final = 2 * x + dz == z
            target = block_rows(block, my_block, t)

            @pl.when(jnp.logical_not(mine) & jnp.logical_not(final))
            def _():
                remote(
                    grad.at[layer], mid.at[slot, dz], sent, relay_sem.at[slot, dz], relay, t
                ).start()

            @pl.when(jnp.logical_not(mine) & final)
            def _():
                remote(grad.at[layer], target, sent, block_sem.at[my_block], relay, t).start()

            @pl.when(mine & jnp.logical_not(final))
            def _():
                remote(grad.at[layer], target, sent, block_sem.at[my_block], layer, x).start()

            @pl.when(mine & final)
            def _():
                pltpu.make_async_copy(grad.at[layer], target, block_sem.at[my_block]).start()

        return carry

    lax.fori_loop(0, 32, scatter_plane, 0)

    pltpu.make_async_copy(row_own, rows.at[t], rows_sem).start()
    for o in range(1, 4):
        remote(row_own, rows.at[t], rows_sent, rows_sem, me, lax.rem(t + o, 4)).start()

    def forward(k, carry):
        kk, source_core = k // 2, lax.rem(core + k, 2)
        a, b = offsets(kk)
        sx, sy = lax.rem(x - a + 4, 4), lax.rem(y - b + 4, 4)
        mine = (sx == x) & (sy == y) & (source_core == core)
        slot = source_core * 16 + kk
        index = zlo * 8 + sy * 2 + source_core
        for dz in range(2):

            @pl.when(jnp.logical_not(mine) & (2 * sx + dz != z))
            def _():
                held = mid.at[slot, dz]
                wait_bytes(held, relay_sem.at[slot, dz])
                remote(
                    held,
                    block_rows(block, index, t),
                    sent,
                    block_sem.at[index],
                    layer_at(x, y, dz, core),
                    sx,
                ).start()

        return carry

    lax.fori_loop(0, 32, forward, 0)

    row_e = jnp.full((1, 256), row_esc[0], F32)
    col_e = jnp.full((1, 256), col_esc[0], F32)
    row_base, col_base = inverse_fourth_root(row_e), inverse_fourth_root(col_e)
    row_coef = inverse_fourth_root(row_eig[...] + row_e) - row_base
    col_coef = inverse_fourth_root(col_eig[...] + col_e) - col_base
    coef_t[...] = jnp.transpose(jnp.broadcast_to(row_coef, (256, 256)))

    wait_bytes(rows, rows_sem)
    for r in range(4):
        rows_t[:, 256 * r : 256 * (r + 1)] = jnp.transpose(rows[r].astype(F32)).astype(BF16)

    middle[...] = jnp.zeros_like(middle)
    grad_acc[...] = jnp.zeros_like(grad_acc)
    shift = lax.rem(x - t + 4, 4)

    def project(i, carry):
        sy = lax.rem(y - shift - i // 2 + 8, 4)
        p = lax.rem(i, 2) * 4 + sy
        for half in range(2):
            wait_bytes(block.at[2 * p + half], block_sem.at[2 * p + half])
        pair = jnp.concatenate([block[2 * p], block[2 * p + 1]], axis=1)
        proj = jnp.dot(rows_t[...], pair, preferred_element_type=F32)
        scaled[p] = (coef_t[...] * proj).astype(BF16)
        column = cols[pl.ds(pl.multiple_of(p * 256, 256), 256), :]
        for r in range(4):
            piece = pair[256 * r : 256 * (r + 1)]
            middle[r] += jnp.dot(piece, column, preferred_element_type=F32)
            grad_acc[...] += fold(piece.astype(F32))
        return carry

    lax.fori_loop(0, 8, project, 0)

    for r in range(4):
        mid_send[r] = middle[r].astype(BF16)
    for o in range(1, 4):
        peer = lax.rem(t + o, 4)
        remote(mid_send.at[peer], mid_recv.at[3 - o], part_sent, part_sem, me, peer).start()
    wait_bytes(mid_recv, part_sem)
    total = middle[t]
    for o in range(3):
        total = total + mid_recv[o].astype(F32)
    mid_all[t] = total.astype(BF16)
    for o in range(1, 4):
        peer = lax.rem(t + o, 4)
        remote(mid_all.at[t], mid_all.at[t], full_sent, full_sem, me, peer).start()
    wait_bytes(mid_recv, full_sem)

    core_mat = jnp.zeros((256, 256), F32)
    for r in range(4):
        core_mat += jnp.dot(
            rows_t[:, 256 * r : 256 * (r + 1)], mid_all[r], preferred_element_type=F32
        )
    core_mat = (coef_t[...] * core_mat).astype(BF16)
    for r in range(4):
        mixed = row_base * mid_all[r].astype(F32) + jnp.dot(
            rows[r], core_mat, preferred_element_type=F32
        )
        left[r] = (mixed * col_coef).astype(BF16)

    both_base = row_base * col_base
    norm_send[0] = grad_acc[...]
    norm_send[1] = jnp.zeros((8, 128), F32)

    def update(p, carry):
        column = cols[pl.ds(pl.multiple_of(p * 256, 256), 256), :]
        for r in range(4):
            span = slice(256 * r, 256 * (r + 1))
            value = jnp.dot(rows[r], scaled[p], preferred_element_type=F32) * col_base
            value += lax.dot_general(
                left[r], column, (((1,), (1,)), ((), ())), preferred_element_type=F32
            )
            held = jnp.concatenate([block[2 * p, span], block[2 * p + 1, span]], axis=1)
            value += both_base * held.astype(F32)
            raw[p, span] = value
            norm_send[1] += fold(value)
        return carry

    lax.fori_loop(0, 8, update, 0)

    for o in range(1, 4):
        remote(
            norm_send, norm_recv.at[3 - o], norm_sent, norm_sem, me, lax.rem(t + o, 4)
        ).start()
    wait_bytes(norm_recv, norm_sem)
    sums = norm_send[...] + norm_recv[0] + norm_recv[1] + norm_recv[2]
    grad_sq = jnp.sum(sums[0], keepdims=True)
    update_sq = jnp.sum(sums[1], keepdims=True)
    factor = jnp.sqrt((grad_sq + 1.0) / (update_sq + 1.0))

    def give(i, carry):
        def order(k):
            return lax.rem(zlo + k, 2) * 4 + lax.rem(y + k // 2, 4)

        @pl.when(i < 8)
        def _():
            p = order(i)
            for half in range(2):
                ready[2 * p + half] = (
                    raw[p, :, 128 * half : 128 * (half + 1)] * factor
                ).astype(BF16)

        @pl.when(i > 0)
        def _():
            p = order(i - 1)
            for h in range(2):
                index = 2 * p + lax.rem(core + h, 2)
                layer = t * 16 + index
                for o in range(4):
                    part = lax.rem(t + o + 1, 4)
                    piece = block_rows(ready, index, part)
                    own = (layer == me) & (part == t)

                    @pl.when(jnp.logical_not(own))
                    def _():
                        remote(piece, out.at[me], out_sent, out_sem, layer, part).start()

                    @pl.when(own)
                    def _():
                        pltpu.make_async_copy(piece, out.at[me], out_sem).start()

        return carry

    lax.fori_loop(0, 9, give, 0)

    wait_bytes(raw.at[pl.ds(0, 7)], sent)
    wait_bytes(raw.at[7, pl.ds(0, 384)], sent)
    wait_bytes(rows.at[pl.ds(0, 3)], rows_sent)
    wait_bytes(mid_recv, part_sent)
    wait_bytes(mid_recv, full_sent)
    wait_bytes(norm_recv, norm_sent)

    @pl.when(home)
    def _():
        wait_bytes(out.at[pl.ds(0, 63)], out_sent)

    @pl.when(jnp.logical_not(home))
    def _():
        wait_bytes(out, out_sent)

    wait_bytes(out, out_sem)


def body(gradient, row_basis, column_basis, row_eigen, column_eigen, row_escape, column_escape):
    dma = pltpu.SemaphoreType.DMA
    vmem = pl.BlockSpec(memory_space=pltpu.VMEM)
    smem = pl.BlockSpec(memory_space=pltpu.SMEM)
    hbm = pl.BlockSpec(memory_space=pltpu.HBM)
    return pl.pallas_call(
        kernel,
        out_shape=jax.ShapeDtypeStruct((64, 256, 128), BF16),
        in_specs=[smem, smem, hbm, hbm, vmem, vmem, vmem],
        out_specs=hbm,
        scratch_shapes=[
            pltpu.VMEM((16, 1024, 128), BF16),
            pltpu.VMEM((32, 2, 256, 128), BF16),
            pltpu.VMEM((4, 256, 256), BF16),
            pltpu.VMEM((256, 1024), BF16),
            pltpu.VMEM((256, 256), F32),
            pltpu.VMEM((8, 256, 256), BF16),
            pltpu.VMEM((4, 256, 256), F32),
            pltpu.VMEM((4, 256, 256), BF16),
            pltpu.VMEM((3, 256, 256), BF16),
            pltpu.VMEM((4, 256, 256), BF16),
            pltpu.VMEM((4, 256, 256), BF16),
            pltpu.VMEM((8, 1024, 256), F32),
            pltpu.VMEM((16, 1024, 128), BF16),
            pltpu.VMEM((2, 8, 128), F32),
            pltpu.VMEM((3, 2, 8, 128), F32),
            pltpu.VMEM((8, 128), F32),
            dma,
            dma((32, 2)),
            dma((16,)),
            dma,
            dma,
            dma,
            dma,
            dma,
            dma,
            dma,
            dma,
            dma,
            dma,
        ],
        compiler_params=pltpu.CompilerParams(
            collective_id=0, has_side_effects=True, vmem_limit_bytes=56 * 1024 * 1024
        ),
        name="sketchy",
    )(
        row_escape,
        column_escape,
        gradient,
        row_basis.reshape(256, 256),
        column_basis.reshape(2048, 256),
        row_eigen,
        column_eigen,
    )


def solution(mesh):
    in_specs = (
        P(None, "tensor", "layer"),
        P("layer", "tensor", None),
        P("layer", "tensor", None),
        P("layer", None),
        P("layer", None),
        P("layer"),
        P("layer"),
    )
    out_specs = P(None, "tensor", "layer")
    return jax.shard_map(body, mesh=mesh, in_specs=in_specs, out_specs=out_specs, check_vma=False)
```

time: 507 us -> 255 us (0.50)
  Pallas kernels: 0 us -> 246 us
  waiting for transfers between devices: 213 us -> 0 us
  blocking collectives: 141 us -> 0 us
  starting transfers between devices: 67.6 us -> 0 us
  matrix products: 29 us -> 0 us
  local copies, waits for them, and re-layouts: 21.1 us -> 4.7 us
  other arithmetic: 15.2 us -> 0 us
  between operations: 16.3 us -> 1.3 us
    pallas_call x0 -> x1, Pallas kernels: none -> 246 us  [body(): pl.pallas_call(kernel, out_shape=jax.ShapeDtypeStruct((64, 256, 128), BF1...]
    all_to_all x3 -> x0, blocking collectives: 130 us -> none  [the longest x2 71.8 us: cut_exchange(): lax.all_to_all(section, axis, split_axis=0, concat_axis=0, tiled=True)]
    reduce_scatter x1 -> x0, waiting for transfers between devices: 107 us -> none  [body(): lax.psum_scatter(jnp.einsum('lrk,lrd->dlk', row_basis, group_block, prefe...]
    all_to_all x2 -> x0, starting transfers between devices: 67.6 us -> none  [from_everyone(): return lax.all_to_all(copies, axis, split_axis=0, concat_axis=0, tiled=True)]
    psum x1 -> x0, waiting for transfers between devices: 54.9 us -> none  [body(): core_mat = lax.psum(core_part.astype(jnp.bfloat16), 'tensor')]
    all_to_all x2 -> x0, waiting for transfers between devices: 50.8 us -> none  [from_everyone(): return lax.all_to_all(copies, axis, split_axis=0, concat_axis=0, tiled=True)]
    dot_general x5 -> x0, matrix products: 29 us -> none  [the longest x1 11 us: body(): jnp.einsum('lrk,ldk->lrd', left_factor, whole_columns, preferred_element_...]
    psum x1 -> x0, blocking collectives: 10.5 us -> none  [group_norm(): return lax.psum(partial_sq, 'tensor')]
  transfers between devices with their start and end apart: 4 -> 0, of which waited for: 3 -> 0; matrix products, arithmetic and copies ran while one was open for 4% -> 0% of each run, Pallas kernels for 0% -> 0%
where the time goes in v1:
time: 255 us; the launch traced here: 252 us
  Pallas kernels  246 us (96%)
  local copies, waits for them, and re-layouts  4.7 us (2%)
    pallas_call x1, Pallas kernels, body(): pl.pallas_call(kernel, out_shape=jax.ShapeDtypeStruct((64, 256, 128), BF1...  246 us

profile of v1, /device:TPU:5, one launch (start us, length us, event | category | flops | bytes accessed | tf_op | source)
XLA Modules:
  0.0 252.3 jit_solution(4992575367866410699)
XLA Ops:
  1.3 246.3 %sketchy.1 = bf16[64,256,128]{2,1,0:T(8,128)(2,1)} custom-call(f32[1]{0:T(128)S(6)} %copy.9.row_esc, f32[1]{0:T(128)S(6)} %copy.10.col_esc, bf16[64,256,128]{2,1,0:T(8,128)(2,1)} %grad.1, bf16[256,256]{1,0:T(8,128)(2,1)} %bitcast.3, bf16[2048,256]{1,0:T(8,128)(2,1)} %bitcast.2, f32[1,256]{1,0:T(1,128)} %row_eig.1, f32[1,256]{1,0:T(1,128)} %col_eig.1), custom_call_target="tpu_custom_call" | custom-call | tf_op jit(solution)/shard_map/sketchy/pallas_call | solution.py:331
  247.6 4.7 %copy.11 = bf16[64,256,128]{2,1,0:T(8,128)(2,1)} copy(bf16[64,256,128]{2,1,0:T(8,128)(2,1)} %sketchy.1) | data formatting | bytes 8388608

commit v2 on v1

--- a/solution.py
+++ b/solution.py
@@ -6,6 +6,8 @@
 from jax.sharding import PartitionSpec as P
 
 MESH = pl.DeviceIdType.MESH
+GO_AFTER = 4
+EARLY, LATE = 2, 6
 F32 = jnp.float32
 BF16 = jnp.bfloat16
 
@@ -44,7 +46,7 @@
     col_esc,
     grad,
     row_own,
-    cols,
+    cols_in,
     row_eig,
     col_eig,
     out,
@@ -55,15 +57,19 @@
     coef_t,
     scaled,
     middle,
+    mid_far,
+    mid_via,
     mid_send,
     mid_recv,
     mid_all,
     left,
-    raw,
     ready,
+    factor_out,
+    factor_in,
     norm_send,
     norm_recv,
     grad_acc,
+    cols,
     sent,
     relay_sem,
     block_sem,
@@ -77,6 +83,17 @@
     norm_sent,
     out_sem,
     out_sent,
+    factor_sem,
+    factor_sent,
+    go_sem,
+    cols_sem,
+    own_sem,
+    rows_last,
+    rows_sent2,
+    far_sem,
+    far_sent,
+    full_last,
+    full_sent2,
 ):
     me, t = lax.axis_index("layer"), lax.axis_index("tensor")
     x, zlo, y, core = me // 16, lax.rem(me // 8, 2), lax.rem(me // 2, 4), lax.rem(me, 2)
@@ -109,6 +126,28 @@
     lax.fori_loop(1, 32, greet_plane, 0)
     lax.fori_loop(1, 8, greet_ring, 0)
     pl.semaphore_wait(barrier, 38)
+
+    up, down, across = lax.rem(t + 1, 4), lax.rem(t + 3, 4), lax.rem(t + 2, 4)
+
+    def pass_round(source, blocks, first, second, first_sent, second_sent):
+        remote(source, blocks.at[t], first_sent, first.at[0], me, up).start()
+        remote(source, blocks.at[t], first_sent, first.at[1], me, down).start()
+
+        def pass_on():
+            wait_bytes(blocks.at[down], first.at[0])
+            half = blocks.at[down, pl.ds(0, 128)]
+            remote(half, half, second_sent, second, me, up).start()
+            wait_bytes(blocks.at[up], first.at[1])
+            half = blocks.at[up, pl.ds(128, 128)]
+            remote(half, half, second_sent, second, me, down).start()
+
+        return pass_on
+
+    own_rows = pltpu.make_async_copy(row_own, rows.at[t], own_sem)
+    own_rows.start()
+    pass_rows_on = pass_round(row_own, rows, rows_sem, rows_last, rows_sent, rows_sent2)
+
+    pltpu.make_async_copy(cols_in, cols, cols_sem).start()
 
     def offsets(k):
         a = lax.rem(k + 1, 4)
@@ -150,10 +189,6 @@
         return carry
 
     lax.fori_loop(0, 32, scatter_plane, 0)
-
-    pltpu.make_async_copy(row_own, rows.at[t], rows_sem).start()
-    for o in range(1, 4):
-        remote(row_own, rows.at[t], rows_sent, rows_sem, me, lax.rem(t + o, 4)).start()
 
     def forward(k, carry):
         kk, source_core = k // 2, lax.rem(core + k, 2)
@@ -179,7 +214,13 @@
 
         return carry
 
-    lax.fori_loop(0, 32, forward, 0)
+    lax.fori_loop(0, (1 - core) * 8, forward, 0)
+    pass_rows_on()
+    @pl.when(core == 1)
+    def _():
+        pl.semaphore_wait(go_sem, 1)
+
+    lax.fori_loop((1 - core) * 8, 32, forward, 0)
 
     row_e = jnp.full((1, 256), row_esc[0], F32)
     col_e = jnp.full((1, 256), col_esc[0], F32)
@@ -188,7 +229,9 @@
     col_coef = inverse_fourth_root(col_eig[...] + col_e) - col_base
     coef_t[...] = jnp.transpose(jnp.broadcast_to(row_coef, (256, 256)))
 
-    wait_bytes(rows, rows_sem)
+    own_rows.wait()
+    wait_bytes(rows.at[across], rows_last)
+    wait_bytes(cols, cols_sem)
     for r in range(4):
         rows_t[:, 256 * r : 256 * (r + 1)] = jnp.transpose(rows[r].astype(F32)).astype(BF16)
 
@@ -209,24 +252,32 @@
             piece = pair[256 * r : 256 * (r + 1)]
             middle[r] += jnp.dot(piece, column, preferred_element_type=F32)
             grad_acc[...] += fold(piece.astype(F32))
+
+        @pl.when((core == 0) & (i == GO_AFTER))
+        def _():
+            pl.semaphore_signal(go_sem, inc=1, device_id=(me + 1, t), device_id_type=MESH)
+
         return carry
 
     lax.fori_loop(0, 8, project, 0)
 
-    for r in range(4):
-        mid_send[r] = middle[r].astype(BF16)
-    for o in range(1, 4):
-        peer = lax.rem(t + o, 4)
-        remote(mid_send.at[peer], mid_recv.at[3 - o], part_sent, part_sem, me, peer).start()
+    far = middle[across].astype(BF16)
+    mid_far[...] = far
+    remote(mid_far.at[pl.ds(0, 128)], mid_via.at[0], far_sent, far_sem.at[0], me, down).start()
+    remote(mid_far.at[pl.ds(128, 128)], mid_via.at[1], far_sent, far_sem.at[1], me, up).start()
+    wait_bytes(mid_via.at[0], far_sem.at[0])
+    wait_bytes(mid_via.at[1], far_sem.at[1])
+    mid_send[0, 0:128] = (middle[down, 0:128] + mid_via[0].astype(F32)).astype(BF16)
+    mid_send[0, 128:256] = middle[down, 128:256].astype(BF16)
+    mid_send[1, 0:128] = middle[up, 0:128].astype(BF16)
+    mid_send[1, 128:256] = (middle[up, 128:256] + mid_via[1].astype(F32)).astype(BF16)
+    remote(mid_send.at[0], mid_recv.at[0], part_sent, part_sem, me, down).start()
+    remote(mid_send.at[1], mid_recv.at[1], part_sent, part_sem, me, up).start()
     wait_bytes(mid_recv, part_sem)
-    total = middle[t]
-    for o in range(3):
-        total = total + mid_recv[o].astype(F32)
-    mid_all[t] = total.astype(BF16)
-    for o in range(1, 4):
-        peer = lax.rem(t + o, 4)
-        remote(mid_all.at[t], mid_all.at[t], full_sent, full_sem, me, peer).start()
-    wait_bytes(mid_recv, full_sem)
+    mid_all[t] = (middle[t] + mid_recv[0].astype(F32) + mid_recv[1].astype(F32)).astype(BF16)
+    pass_middle_on = pass_round(mid_all.at[t], mid_all, full_sem, full_last, full_sent, full_sent2)
+    pass_middle_on()
+    wait_bytes(mid_all.at[across], full_last)
 
     core_mat = jnp.zeros((256, 256), F32)
     for r in range(4):
@@ -244,7 +295,31 @@
     norm_send[0] = grad_acc[...]
     norm_send[1] = jnp.zeros((8, 128), F32)
 
-    def update(p, carry):
+    def order(k):
+        return lax.rem(zlo + k, 2) * 4 + lax.rem(y + k // 2, 4)
+
+    def send_pair(i, carry):
+        p = order(i)
+        for h in range(2):
+            index = 2 * p + lax.rem(core + h, 2)
+            layer = t * 16 + index
+            for o in range(4):
+                part = lax.rem(t + o + 1, 4)
+                piece = block_rows(ready, index, part)
+                own = (layer == me) & (part == t)
+
+                @pl.when(jnp.logical_not(own))
+                def _():
+                    remote(piece, out.at[me], out_sent, out_sem.at[me], layer, part).start()
+
+                @pl.when(own)
+                def _():
+                    pltpu.make_async_copy(piece, out.at[me], out_sem.at[me]).start()
+
+        return carry
+
+    def update(i, carry):
+        p = order(i)
         column = cols[pl.ds(pl.multiple_of(p * 256, 256), 256), :]
         for r in range(4):
             span = slice(256 * r, 256 * (r + 1))
@@ -254,73 +329,82 @@
             )
             held = jnp.concatenate([block[2 * p, span], block[2 * p + 1, span]], axis=1)
             value += both_base * held.astype(F32)
-            raw[p, span] = value
+            ready[2 * p, span] = value[:, :128].astype(BF16)
+            ready[2 * p + 1, span] = value[:, 128:].astype(BF16)
             norm_send[1] += fold(value)
+
+        @pl.when((i > 0) & (i <= EARLY))
+        def _():
+            send_pair(i - 1, 0)
+
         return carry
 
     lax.fori_loop(0, 8, update, 0)
-
     for o in range(1, 4):
         remote(
             norm_send, norm_recv.at[3 - o], norm_sent, norm_sem, me, lax.rem(t + o, 4)
         ).start()
+    lax.fori_loop(EARLY, LATE, send_pair, 0)
     wait_bytes(norm_recv, norm_sem)
     sums = norm_send[...] + norm_recv[0] + norm_recv[1] + norm_recv[2]
     grad_sq = jnp.sum(sums[0], keepdims=True)
     update_sq = jnp.sum(sums[1], keepdims=True)
     factor = jnp.sqrt((grad_sq + 1.0) / (update_sq + 1.0))
+    factor_out[...] = jnp.broadcast_to(factor, (8, 128))
+    wait_bytes(norm_recv, norm_sent)
 
     def give(i, carry):
-        def order(k):
-            return lax.rem(zlo + k, 2) * 4 + lax.rem(y + k // 2, 4)
-
-        @pl.when(i < 8)
+        layer, part = t * 16 + lax.rem(my_block + i // 4, 16), lax.rem(t + i + 1, 4)
+        own = (layer == me) & (part == t)
+
+        @pl.when(jnp.logical_not(own))
         def _():
-            p = order(i)
-            for half in range(2):
-                ready[2 * p + half] = (
-                    raw[p, :, 128 * half : 128 * (half + 1)] * factor
-                ).astype(BF16)
-
-        @pl.when(i > 0)
+            remote(
+                factor_out.at[pl.ds(0, 1)],
+                factor_in.at[me, pl.ds(0, 1)],
+                factor_sent,
+                factor_sem.at[me],
+                layer,
+                part,
+            ).start()
+
+        @pl.when(own)
         def _():
-            p = order(i - 1)
-            for h in range(2):
-                index = 2 * p + lax.rem(core + h, 2)
-                layer = t * 16 + index
-                for o in range(4):
-                    part = lax.rem(t + o + 1, 4)
-                    piece = block_rows(ready, index, part)
-                    own = (layer == me) & (part == t)
-
-                    @pl.when(jnp.logical_not(own))
-                    def _():
-                        remote(piece, out.at[me], out_sent, out_sem, layer, part).start()
-
-                    @pl.when(own)
-                    def _():
-                        pltpu.make_async_copy(piece, out.at[me], out_sem).start()
-
-        return carry
-
-    lax.fori_loop(0, 9, give, 0)
-
-    wait_bytes(raw.at[pl.ds(0, 7)], sent)
-    wait_bytes(raw.at[7, pl.ds(0, 384)], sent)
-    wait_bytes(rows.at[pl.ds(0, 3)], rows_sent)
+            pltpu.make_async_copy(
+                factor_out.at[pl.ds(0, 1)], factor_in.at[me, pl.ds(0, 1)], factor_sem.at[me]
+            ).start()
+
+        return carry
+
+    lax.fori_loop(0, 64, give, 0)
+    lax.fori_loop(LATE, 8, send_pair, 0)
+
+    def scale(i, carry):
+        layer = lax.rem(i, 32) * 2 + i // 32
+        wait_bytes(out.at[layer], out_sem.at[layer])
+        wait_bytes(factor_in.at[layer, pl.ds(0, 1)], factor_sem.at[layer])
+        out[layer] = (out[layer].astype(F32) * factor_in[layer, 0:1]).astype(BF16)
+        return carry
+
+    lax.fori_loop(0, 64, scale, 0)
+    wait_bytes(mid, sent)
+    wait_bytes(mid.at[pl.ds(0, 27)], sent)
+    wait_bytes(rows.at[pl.ds(0, 2)], rows_sent)
+    wait_bytes(rows.at[0], rows_sent2)
+    wait_bytes(mid_far, far_sent)
     wait_bytes(mid_recv, part_sent)
     wait_bytes(mid_recv, full_sent)
-    wait_bytes(norm_recv, norm_sent)
+    wait_bytes(mid_far, full_sent2)
 
     @pl.when(home)
     def _():
         wait_bytes(out.at[pl.ds(0, 63)], out_sent)
+        wait_bytes(factor_in.at[pl.ds(0, 63), pl.ds(0, 1)], factor_sent)
 
     @pl.when(jnp.logical_not(home))
     def _():
         wait_bytes(out, out_sent)
-
-    wait_bytes(out, out_sem)
+        wait_bytes(factor_in.at[:, pl.ds(0, 1)], factor_sent)
 
 
 def body(gradient, row_basis, column_basis, row_eigen, column_eigen, row_escape, column_escape):
@@ -330,9 +414,9 @@
     hbm = pl.BlockSpec(memory_space=pltpu.HBM)
     return pl.pallas_call(
         kernel,
-        out_shape=jax.ShapeDtypeStruct((64, 256, 128), BF16),
-        in_specs=[smem, smem, hbm, hbm, vmem, vmem, vmem],
-        out_specs=hbm,
+        out_shape=pltpu.VMEM((64, 256, 128), BF16),
+        in_specs=[smem, smem, hbm, hbm, hbm, vmem, vmem],
+        out_specs=vmem,
         scratch_shapes=[
             pltpu.VMEM((16, 1024, 128), BF16),
             pltpu.VMEM((32, 2, 256, 128), BF16),
@@ -341,25 +425,40 @@
             pltpu.VMEM((256, 256), F32),
             pltpu.VMEM((8, 256, 256), BF16),
             pltpu.VMEM((4, 256, 256), F32),
-            pltpu.VMEM((4, 256, 256), BF16),
-            pltpu.VMEM((3, 256, 256), BF16),
+            pltpu.VMEM((256, 256), BF16),
+            pltpu.VMEM((2, 128, 256), BF16),
+            pltpu.VMEM((2, 256, 256), BF16),
+            pltpu.VMEM((2, 256, 256), BF16),
             pltpu.VMEM((4, 256, 256), BF16),
             pltpu.VMEM((4, 256, 256), BF16),
-            pltpu.VMEM((8, 1024, 256), F32),
             pltpu.VMEM((16, 1024, 128), BF16),
+            pltpu.VMEM((8, 128), F32),
+            pltpu.VMEM((64, 8, 128), F32),
             pltpu.VMEM((2, 8, 128), F32),
             pltpu.VMEM((3, 2, 8, 128), F32),
             pltpu.VMEM((8, 128), F32),
+            pltpu.VMEM((2048, 256), BF16),
             dma,
             dma((32, 2)),
             dma((16,)),
-            dma,
-            dma,
-            dma,
-            dma,
-            dma,
-            dma,
-            dma,
+            dma((2,)),
+            dma,
+            dma,
+            dma,
+            dma((2,)),
+            dma,
+            dma,
+            dma,
+            dma((64,)),
+            dma,
+            dma((64,)),
+            dma,
+            pltpu.SemaphoreType.REGULAR,
+            dma,
+            dma,
+            dma,
+            dma,
+            dma((2,)),
             dma,
             dma,
             dma,

time: 255 us -> 235 us (0.922)
  Pallas kernels: 246 us -> 230 us
  local copies, waits for them, and re-layouts: 4.7 us -> 2.02 us
    pallas_call x1, Pallas kernels: 246 us -> 230 us  [body(): pl.pallas_call(kernel, out_shape=pltpu.VMEM((64, 256, 128), BF16), in_spe...]
    unnamed x1, local copies, waits for them, and re-layouts: 4.7 us -> 2.02 us
where the time goes in v2:
time: 235 us; the launch traced here: 233 us
  Pallas kernels  230 us (98%)
    pallas_call x1, Pallas kernels, body(): pl.pallas_call(kernel, out_shape=pltpu.VMEM((64, 256, 128), BF16), in_spe...  230 us

profile of v2, /device:TPU:5, one launch (start us, length us, event | category | flops | bytes accessed | tf_op | source)
XLA Modules:
  0.0 233.0 jit_solution(12174061873550085982)
XLA Ops:
  1.3 229.7 %sketchy.1 = bf16[64,256,128]{2,1,0:T(8,128)(2,1)S(1)} custom-call(f32[1]{0:T(128)S(6)} %copy.10.row_esc, f32[1]{0:T(128)S(6)} %copy.11.col_esc, bf16[64,256,128]{2,1,0:T(8,128)(2,1)} %grad.1, bf16[256,256]{1,0:T(8,128)(2,1)} %bitcast.3, bf16[2048,256]{1,0:T(8,128)(2,1)} %bitcast.2, f32[1,256]{1,0:T(1,128)} %row_eig.1, f32[1,256]{1,0:T(1,128)} %col_eig.1), custom_call_target="tpu_custom_call" | custom-call | tf_op jit(solution)/shard_map/sketchy/pallas_call | solution.py:415
  231.0 2.0 copy.9

commit v3 on v2

--- a/solution.py
+++ b/solution.py
@@ -7,7 +7,7 @@
 
 MESH = pl.DeviceIdType.MESH
 GO_AFTER = 4
-EARLY, LATE = 2, 6
+EARLY, LATE = 3, 7
 F32 = jnp.float32
 BF16 = jnp.bfloat16
 
@@ -42,13 +42,13 @@
 
 
 def kernel(
-    row_esc,
-    col_esc,
+    row_esc_in,
+    col_esc_in,
     grad,
     row_own,
     cols_in,
-    row_eig,
-    col_eig,
+    row_eig_in,
+    col_eig_in,
     out,
     block,
     mid,
@@ -70,6 +70,10 @@
     norm_recv,
     grad_acc,
     cols,
+    row_esc,
+    col_esc,
+    row_eig,
+    col_eig,
     sent,
     relay_sem,
     block_sem,
@@ -94,12 +98,14 @@
     far_sent,
     full_last,
     full_sent2,
+    small_sem,
 ):
     me, t = lax.axis_index("layer"), lax.axis_index("tensor")
     x, zlo, y, core = me // 16, lax.rem(me // 8, 2), lax.rem(me // 2, 4), lax.rem(me, 2)
     z = 2 * t + zlo
     my_block = lax.rem(me, 16)
     home = t == x
+    my_group = ((1 - core) * 4 + x) * 2 + zlo
 
     barrier = pltpu.get_barrier_semaphore()
 
@@ -123,8 +129,8 @@
         )
         return carry
 
-    lax.fori_loop(1, 32, greet_plane, 0)
-    lax.fori_loop(1, 8, greet_ring, 0)
+    lax.fori_loop(1, 8, greet_ring, 0, unroll=True)
+    lax.fori_loop(1, 32, greet_plane, 0, unroll=True)
     pl.semaphore_wait(barrier, 38)
 
     up, down, across = lax.rem(t + 1, 4), lax.rem(t + 3, 4), lax.rem(t + 2, 4)
@@ -148,6 +154,10 @@
     pass_rows_on = pass_round(row_own, rows, rows_sem, rows_last, rows_sent, rows_sent2)
 
     pltpu.make_async_copy(cols_in, cols, cols_sem).start()
+    small = [(row_esc_in, row_esc), (col_esc_in, col_esc), (row_eig_in, row_eig), (col_eig_in, col_eig)]
+    small = [pltpu.make_async_copy(a, b, small_sem.at[i]) for i, (a, b) in enumerate(small)]
+    for copy in small:
+        copy.start()
 
     def offsets(k):
         a = lax.rem(k + 1, 4)
@@ -157,7 +167,7 @@
         return ref.at[index, pl.ds(pl.multiple_of(part * 256, 256), 256)]
 
     def scatter_plane(k, carry):
-        kk, dest_core = lax.rem(k, 16), k // 16
+        kk, dest_core = lax.rem(k, 16), 1 - k // 16
         a, b = offsets(kk)
         dx, dy = lax.rem(x + a, 4), lax.rem(y + b, 4)
         mine = (dx == x) & (dy == y) & (dest_core == core)
@@ -214,16 +224,18 @@
 
         return carry
 
-    lax.fori_loop(0, (1 - core) * 8, forward, 0)
+    lax.fori_loop(0, core * 8, forward, 0)
     pass_rows_on()
-    @pl.when(core == 1)
+    @pl.when(core == 0)
     def _():
         pl.semaphore_wait(go_sem, 1)
 
-    lax.fori_loop((1 - core) * 8, 32, forward, 0)
-
-    row_e = jnp.full((1, 256), row_esc[0], F32)
-    col_e = jnp.full((1, 256), col_esc[0], F32)
+    lax.fori_loop(core * 8, 32, forward, 0)
+
+    for copy in small:
+        copy.wait()
+    row_e = jnp.broadcast_to(row_esc[...], (1, 256))
+    col_e = jnp.broadcast_to(col_esc[...], (1, 256))
     row_base, col_base = inverse_fourth_root(row_e), inverse_fourth_root(col_e)
     row_coef = inverse_fourth_root(row_eig[...] + row_e) - row_base
     col_coef = inverse_fourth_root(col_eig[...] + col_e) - col_base
@@ -253,9 +265,9 @@
             middle[r] += jnp.dot(piece, column, preferred_element_type=F32)
             grad_acc[...] += fold(piece.astype(F32))
 
-        @pl.when((core == 0) & (i == GO_AFTER))
+        @pl.when((core == 1) & (i == GO_AFTER))
         def _():
-            pl.semaphore_signal(go_sem, inc=1, device_id=(me + 1, t), device_id_type=MESH)
+            pl.semaphore_signal(go_sem, inc=1, device_id=(me - 1, t), device_id_type=MESH)
 
         return carry
 
@@ -310,11 +322,11 @@
 
                 @pl.when(jnp.logical_not(own))
                 def _():
-                    remote(piece, out.at[me], out_sent, out_sem.at[me], layer, part).start()
+                    remote(piece, out.at[me], out_sent, out_sem.at[my_group], layer, part).start()
 
                 @pl.when(own)
                 def _():
-                    pltpu.make_async_copy(piece, out.at[me], out_sem.at[me]).start()
+                    pltpu.make_async_copy(piece, out.at[me], out_sem.at[my_group]).start()
 
         return carry
 
@@ -363,7 +375,7 @@
                 factor_out.at[pl.ds(0, 1)],
                 factor_in.at[me, pl.ds(0, 1)],
                 factor_sent,
-                factor_sem.at[me],
+                factor_sem.at[core],
                 layer,
                 part,
             ).start()
@@ -371,7 +383,7 @@
         @pl.when(own)
         def _():
             pltpu.make_async_copy(
-                factor_out.at[pl.ds(0, 1)], factor_in.at[me, pl.ds(0, 1)], factor_sem.at[me]
+                factor_out.at[pl.ds(0, 1)], factor_in.at[me, pl.ds(0, 1)], factor_sem.at[core]
             ).start()
 
         return carry
@@ -380,13 +392,17 @@
     lax.fori_loop(LATE, 8, send_pair, 0)
 
     def scale(i, carry):
-        layer = lax.rem(i, 32) * 2 + i // 32
-        wait_bytes(out.at[layer], out_sem.at[layer])
-        wait_bytes(factor_in.at[layer, pl.ds(0, 1)], factor_sem.at[layer])
-        out[layer] = (out[layer].astype(F32) * factor_in[layer, 0:1]).astype(BF16)
-        return carry
-
-    lax.fori_loop(0, 64, scale, 0)
+        @pl.when(lax.rem(i, 8) == 0)
+        def _():
+            wait_bytes(factor_in.at[pl.ds(0, 32), pl.ds(0, 1)], factor_sem.at[1 - i // 8])
+
+        wait_bytes(out.at[pl.ds(0, 4)], out_sem.at[i])
+        for j in range(4):
+            layer = layer_at(lax.rem(i // 2, 4), j, lax.rem(i, 2), 1 - i // 8)
+            out[layer] = (out[layer].astype(F32) * factor_in[layer, 0:1]).astype(BF16)
+        return carry
+
+    lax.fori_loop(0, 16, scale, 0)
     wait_bytes(mid, sent)
     wait_bytes(mid.at[pl.ds(0, 27)], sent)
     wait_bytes(rows.at[pl.ds(0, 2)], rows_sent)
@@ -410,12 +426,11 @@
 def body(gradient, row_basis, column_basis, row_eigen, column_eigen, row_escape, column_escape):
     dma = pltpu.SemaphoreType.DMA
     vmem = pl.BlockSpec(memory_space=pltpu.VMEM)
-    smem = pl.BlockSpec(memory_space=pltpu.SMEM)
     hbm = pl.BlockSpec(memory_space=pltpu.HBM)
     return pl.pallas_call(
         kernel,
         out_shape=pltpu.VMEM((64, 256, 128), BF16),
-        in_specs=[smem, smem, hbm, hbm, hbm, vmem, vmem],
+        in_specs=[hbm] * 7,
         out_specs=vmem,
         scratch_shapes=[
             pltpu.VMEM((16, 1024, 128), BF16),
@@ -438,6 +453,10 @@
             pltpu.VMEM((3, 2, 8, 128), F32),
             pltpu.VMEM((8, 128), F32),
             pltpu.VMEM((2048, 256), BF16),
+            pltpu.VMEM((1, 1), F32),
+            pltpu.VMEM((1, 1), F32),
+            pltpu.VMEM((1, 256), F32),
+            pltpu.VMEM((1, 256), F32),
             dma,
             dma((32, 2)),
             dma((16,)),
@@ -449,9 +468,9 @@
             dma,
             dma,
             dma,
-            dma((64,)),
-            dma,
-            dma((64,)),
+            dma((16,)),
+            dma,
+            dma((2,)),
             dma,
             pltpu.SemaphoreType.REGULAR,
             dma,
@@ -462,14 +481,15 @@
             dma,
             dma,
             dma,
+            dma((4,)),
         ],
         compiler_params=pltpu.CompilerParams(
             collective_id=0, has_side_effects=True, vmem_limit_bytes=56 * 1024 * 1024
         ),
         name="sketchy",
     )(
-        row_escape,
-        column_escape,
+        row_escape.reshape(1, 1),
+        column_escape.reshape(1, 1),
         gradient,
         row_basis.reshape(256, 256),
         column_basis.reshape(2048, 256),

time: 235 us -> 231 us (0.983)
  Pallas kernels: 230 us -> 227 us
    pallas_call x1, Pallas kernels: 230 us -> 227 us  [body(): pl.pallas_call(kernel, out_shape=pltpu.VMEM((64, 256, 128), BF16), in_spe...]
where the time goes in v3:
time: 231 us
  Pallas kernels  227 us (98%)
    pallas_call x1, Pallas kernels, body(): pl.pallas_call(kernel, out_shape=pltpu.VMEM((64, 256, 128), BF16), in_spe...  227 us

profile of v3, /device:TPU:5, one launch (start us, length us, event | category | flops | bytes accessed | tf_op | source)
XLA Modules:
  0.0 230.5 jit_solution(11259267934082562540)
XLA Ops:
  1.3 227.2 %sketchy.1 = bf16[64,256,128]{2,1,0:T(8,128)(2,1)S(1)} custom-call(f32[1,1]{1,0:T(1,128)} %bitcast.4.row_esc_in, f32[1,1]{1,0:T(1,128)} %bitcast.5.col_esc_in, bf16[64,256,128]{2,1,0:T(8,128)(2,1)} %grad.1, bf16[256,256]{1,0:T(8,128)(2,1)} %bitcast.7, bf16[2048,256]{1,0:T(8,128)(2,1)} %bitcast.6, f32[1,256]{1,0:T(1,128)} %row_eig_in.1, f32[1,256]{1,0:T(1,128)} %col_eig_in.1), custom_call_target="tpu_custom_call" | custom-call | tf_op jit(solution)/shard_map/sketchy/pallas_call | solution.py:430
  228.5 2.0 copy.9

commit v4 on v3

--- a/solution.py
+++ b/solution.py
@@ -273,32 +273,45 @@
 
     lax.fori_loop(0, 8, project, 0)
 
-    far = middle[across].astype(BF16)
-    mid_far[...] = far
-    remote(mid_far.at[pl.ds(0, 128)], mid_via.at[0], far_sent, far_sem.at[0], me, down).start()
-    remote(mid_far.at[pl.ds(128, 128)], mid_via.at[1], far_sent, far_sem.at[1], me, up).start()
-    wait_bytes(mid_via.at[0], far_sem.at[0])
-    wait_bytes(mid_via.at[1], far_sem.at[1])
-    mid_send[0, 0:128] = (middle[down, 0:128] + mid_via[0].astype(F32)).astype(BF16)
-    mid_send[0, 128:256] = middle[down, 128:256].astype(BF16)
-    mid_send[1, 0:128] = middle[up, 0:128].astype(BF16)
-    mid_send[1, 128:256] = (middle[up, 128:256] + mid_via[1].astype(F32)).astype(BF16)
-    remote(mid_send.at[0], mid_recv.at[0], part_sent, part_sem, me, down).start()
-    remote(mid_send.at[1], mid_recv.at[1], part_sent, part_sem, me, up).start()
-    wait_bytes(mid_recv, part_sem)
-    mid_all[t] = (middle[t] + mid_recv[0].astype(F32) + mid_recv[1].astype(F32)).astype(BF16)
-    pass_middle_on = pass_round(mid_all.at[t], mid_all, full_sem, full_last, full_sent, full_sent2)
-    pass_middle_on()
-    wait_bytes(mid_all.at[across], full_last)
+    spans = (slice(0, 128), slice(128, 256))
+    for h in range(2):
+        mid_far[h] = middle[across, :, spans[h]].astype(BF16)
+        mid_send[h, 0, 128:256] = middle[down, 128:256, spans[h]].astype(BF16)
+        mid_send[h, 1, 0:128] = middle[up, 0:128, spans[h]].astype(BF16)
+        for d, peer in ((0, down), (1, up)):
+            half = mid_far.at[h, pl.ds(128 * d, 128)]
+            remote(half, mid_via.at[h, d], far_sent, far_sem.at[h, d], me, peer).start()
+    for h in range(2):
+        wait_bytes(mid_via.at[h, 0], far_sem.at[h, 0])
+        wait_bytes(mid_via.at[h, 1], far_sem.at[h, 1])
+        mid_send[h, 0, 0:128] = (middle[down, 0:128, spans[h]] + mid_via[h, 0].astype(F32)).astype(BF16)
+        mid_send[h, 1, 128:256] = (middle[up, 128:256, spans[h]] + mid_via[h, 1].astype(F32)).astype(BF16)
+        for d, peer in ((0, down), (1, up)):
+            remote(mid_send.at[h, d], mid_recv.at[h, d], part_sent, part_sem.at[h], me, peer).start()
+    finish = []
+    for h in range(2):
+        wait_bytes(mid_recv.at[h], part_sem.at[h])
+        total = middle[t, :, spans[h]] + mid_recv[h, 0].astype(F32) + mid_recv[h, 1].astype(F32)
+        mid_all[h, t] = total.astype(BF16)
+        finish.append(
+            pass_round(
+                mid_all.at[h, t], mid_all.at[h], full_sem.at[h], full_last.at[h], full_sent, full_sent2
+            )
+        )
+    for pass_middle_on in finish:
+        pass_middle_on()
+    for h in range(2):
+        wait_bytes(mid_all.at[h, across], full_last.at[h])
+    whole = [jnp.concatenate([mid_all[0, r], mid_all[1, r]], axis=1) for r in range(4)]
 
     core_mat = jnp.zeros((256, 256), F32)
     for r in range(4):
         core_mat += jnp.dot(
-            rows_t[:, 256 * r : 256 * (r + 1)], mid_all[r], preferred_element_type=F32
+            rows_t[:, 256 * r : 256 * (r + 1)], whole[r], preferred_element_type=F32
         )
     core_mat = (coef_t[...] * core_mat).astype(BF16)
     for r in range(4):
-        mixed = row_base * mid_all[r].astype(F32) + jnp.dot(
+        mixed = row_base * whole[r].astype(F32) + jnp.dot(
             rows[r], core_mat, preferred_element_type=F32
         )
         left[r] = (mixed * col_coef).astype(BF16)
@@ -440,11 +453,11 @@
             pltpu.VMEM((256, 256), F32),
             pltpu.VMEM((8, 256, 256), BF16),
             pltpu.VMEM((4, 256, 256), F32),
-            pltpu.VMEM((256, 256), BF16),
-            pltpu.VMEM((2, 128, 256), BF16),
-            pltpu.VMEM((2, 256, 256), BF16),
-            pltpu.VMEM((2, 256, 256), BF16),
-            pltpu.VMEM((4, 256, 256), BF16),
+            pltpu.VMEM((2, 256, 128), BF16),
+            pltpu.VMEM((2, 2, 128, 128), BF16),
+            pltpu.VMEM((2, 2, 256, 128), BF16),
+            pltpu.VMEM((2, 2, 256, 128), BF16),
+            pltpu.VMEM((2, 4, 256, 128), BF16),
             pltpu.VMEM((4, 256, 256), BF16),
             pltpu.VMEM((16, 1024, 128), BF16),
             pltpu.VMEM((8, 128), F32),
@@ -462,10 +475,10 @@
             dma((16,)),
             dma((2,)),
             dma,
-            dma,
-            dma,
             dma((2,)),
             dma,
+            dma((2, 2)),
+            dma,
             dma,
             dma,
             dma((16,)),
@@ -477,9 +490,9 @@
             dma,
             dma,
             dma,
+            dma((2, 2)),
+            dma,
             dma((2,)),
-            dma,
-            dma,
             dma,
             dma((4,)),
         ],

time: 231 us -> 230 us (level)
  no operation moved by 1% of the time
where the time goes in v4:
time: 230 us
  Pallas kernels  226 us (98%)
    pallas_call x1, Pallas kernels, body(): pl.pallas_call(kernel, out_shape=pltpu.VMEM((64, 256, 128), BF16), in_spe...  226 us

profile of v4, /device:TPU:5, one launch (start us, length us, event | category | flops | bytes accessed | tf_op | source)
XLA Modules:
  0.0 229.6 jit_solution(10032763001417905643)
XLA Ops:
  1.3 226.3 %sketchy.1 = bf16[64,256,128]{2,1,0:T(8,128)(2,1)S(1)} custom-call(f32[1,1]{1,0:T(1,128)} %bitcast.4.row_esc_in, f32[1,1]{1,0:T(1,128)} %bitcast.5.col_esc_in, bf16[64,256,128]{2,1,0:T(8,128)(2,1)} %grad.1, bf16[256,256]{1,0:T(8,128)(2,1)} %bitcast.7, bf16[2048,256]{1,0:T(8,128)(2,1)} %bitcast.6, f32[1,256]{1,0:T(1,128)} %row_eig_in.1, f32[1,256]{1,0:T(1,128)} %col_eig_in.1), custom_call_target="tpu_custom_call" | custom-call | tf_op jit(solution)/shard_map/sketchy/pallas_call | solution.py:443
  227.6 2.0 copy.9
